TPU v7x, 32 devices: a whole 2x2x4 slice. The times are simulated.
32 devices in a mesh: pole: 4 (over x, core), row: 4 (over z), col: 2 (over y).
Axes of the slice: x: 2, y: 2, z: 4, core: 2. Of those that a mesh axis runs over, the one named last changes fastest.
Arguments:
- anc_inverse: bfloat16 [4, 2, 4, 192, 768], P('pole', None, None, 'col', 'row'), may hold values from -6 to 6
- panel: bfloat16 [4, 2, 768, 1024], P('pole', None, ('row', 'col')), may hold values from -0.21875 to 0.21875
- pattern: int32 [8, 2], replicated, may hold values 0 or 1
- diag_inverse: bfloat16 [4, 2, 1024, 512], P('pole', None, 'col', 'row'), may hold values from -6 to 6
- pole_weights: float32 [4, 2], P('pole'), may hold values from -4 to 4
Outputs:
- inv_panel: float32 [4, 2, 768, 1024], P('pole', None, 'row', 'col')
- inv_diag: bfloat16 [4, 2, 1024, 512], P('pole', None, 'col', 'row')
- density: float32 [1024, 512], P('col', 'row')
All inputs are finite; a program needn't handle non-finite values.
Results may differ from a plain program's by a relative error of at most 0.013.
Values may be sent and summed in bfloat16 or wider, within the bound.
A program may use at most 128 MiB of HBM per device.

v0:
```python
import jax
import jax.numpy as jnp
from jax import lax
from jax.sharding import PartitionSpec as P


def complex_left(left_re, left_im, right_re, right_im):
    upper = jnp.concatenate([left_re, left_im], axis=1)
    lower = jnp.concatenate([-left_im, left_re], axis=1)
    left_side = jnp.concatenate([upper, lower], axis=0)
    right_side = jnp.concatenate([right_re, right_im], axis=0)
    product = lax.dot_general(
        left_side, right_side, (((0,), (0,)), ((), ())), preferred_element_type=jnp.float32
    )
    return product.reshape(2, left_re.shape[1], right_re.shape[1])


def body(anc_inverse, panel, pattern, diag_inverse, pole_weights):
    n_row = lax.axis_size("row")
    n_col = lax.axis_size("col")
    fine_block = lax.axis_index("row") * n_col + lax.axis_index("col")
    pattern_row = lax.dynamic_slice_in_dim(pattern, fine_block, 1, 0)
    block_rows = panel.shape[2]
    width_all = panel.shape[3]
    groups = pattern.shape[1]
    keep_mask = pattern_row.astype(jnp.bfloat16).reshape(1, 1, 1, groups, 1)
    masked = (panel.reshape(1, 2, block_rows, groups, width_all // groups) * keep_mask).reshape(
        1, 2, block_rows, width_all
    )
    local_rows = lax.all_to_all(masked, "col", split_axis=3, concat_axis=2, tiled=True)
    row_count = anc_inverse.shape[4]
    col_count = local_rows.shape[3]
    full_cols = lax.all_gather(local_rows, "row", axis=2, tiled=True)
    stacked = full_cols[0].reshape(2, n_row, block_rows * n_col, col_count)
    segment = lax.all_gather(anc_inverse, "col", axis=3, tiled=True)
    length = segment.shape[3]
    left_side = segment[0].reshape(2, n_row * length, row_count)
    right_side = stacked.reshape(2, n_row * length, col_count)
    summed = complex_left(left_side[0], left_side[1], right_side[0], right_side[1])
    result_panel = -summed
    rounded = result_panel.astype(jnp.bfloat16)
    diag_terms = complex_left(local_rows[0, 0], local_rows[0, 1], rounded[0], rounded[1])
    row_share = lax.psum_scatter(diag_terms, "row", scatter_dimension=2, tiled=True)
    inverse_diag = diag_inverse[0].astype(jnp.float32) - row_share
    pole_weight = pole_weights[0]
    density_term = pole_weight[0] * inverse_diag[1] + pole_weight[1] * inverse_diag[0]
    density = lax.psum(density_term.astype(jnp.bfloat16), "pole").astype(jnp.float32)
    return (result_panel[None], inverse_diag.astype(jnp.bfloat16)[None], density)


def solution(mesh):
    placed = (
        P("pole", None, None, "col", "row"),
        P("pole", None, ("row", "col"), None),
        P(),
        P("pole", None, "col", "row"),
        P("pole", None),
    )
    return jax.shard_map(
        body,
        mesh=mesh,
        in_specs=placed,
        out_specs=(P("pole", None, "row", "col"), P("pole", None, "col", "row"), P("col", "row")),
        check_vma=False,
    )
```

profile of v0, /device:TPU:0, one launch (start us, length us, event | category | flops | bytes accessed | tf_op | source)
XLA Modules:
  0.0 151.4 jit_solution(4732061525736366362)
XLA Ops:
  7.2 0.0 all-gather.2.cloned.1.call-start
  7.2 0.9 fusion.26
  8.1 0.1 broadcast_bitcast_fusion
  8.2 1.0 broadcast_multiply_fusion
  9.2 0.4 copy.12
  9.6 12.2 %all_to_all.18 = bf16[1,2,96,1024]{2,1,0,3:T(2,128)(2,1)S(1)} all-to-all(bf16[1,2,96,1024]{2,1,0,3:T(2,128)(2,1)S(1)} %copy.12), channel_id=1, replica_groups=mesh['pole'=4,'row'=4,'col'=2] {'col'}, dimensions={3} | all-to-all | bytes 786432 | tf_op jit(solution)/shard_map/all_to_all | solution.py:30
  21.8 0.8 copy.15
  22.6 0.8 copy.14
  23.4 0.0 reduce-scatter.2.cloned.1.call-start
  23.5 10.5 %all_gather.6 = bf16[1,2,4,192,192]{4,3,2,1,0:T(8,128)(2,1)S(1)} all-gather(bf16[1,2,4,96,192]{4,3,2,1,0:T(8,128)(2,1)S(1)} %copy-done.1), channel_id=1, replica_groups=mesh['pole'=4,'row'=4,'col'=2] {'col'}, dimensions={3}, use_global_device_ids=true | all-gather | bytes 884736 | tf_op jit(solution)/shard_map/all_gather | solution.py:35
  34.0 0.1 fusion.30
  34.1 0.1 bitcast_negate_fusion
  34.2 26.8 %all-gather.2.cloned.1.call-done = bf16[1,2,768,512]{3,2,1,0:T(8,128)(2,1)} async-done(((bf16[1,2,192,512]{3,2,1,0:T(8,128)(2,1)}), bf16[1,2,768,512]{3,2,1,0:T(8,128)(2,1)}) %all-gather.2.cloned.1.call-update) | async-done | bytes 1572880 | tf_op jit(solution)/shard_map/all_gather | solution.py:33
  61.0 1.5 slice_bitcast_fusion.1
  62.5 1.1 fusion.4
  63.6 2.1 %fusion.14 = f32[1024,512]{1,0:T(8,128)} fusion(bf16[192,512]{1,0:T(8,128)(2,1)S(1)} %get-tuple-element.10, bf16[192,512]{1,0:T(8,128)(2,1)S(1)} %fusion.29, bf16[192,512]{1,0:T(8,128)(2,1)S(1)} %get-tuple-element.9, f32[384,512]{1,0:T(8,128)S(1)} %fusion.4), kind=kOutput, calls=%fused_computation.14 | convolution fusion | flops 405995520 | bytes 3473408 | tf_op jit(solution)/shard_map/dot_general | solution.py:12
  65.7 0.0 all-reduce.2.cloned.1.call-start
  65.8 0.6 copy-done.3
  66.3 0.6 fusion.31
  67.0 41.4 %reduce-scatter.2.cloned.1.call-done = f32[2,512,128]{2,1,0:T(8,128)} async-done(((f32[2,512,512]{2,1,0:T(8,128)}), f32[2,512,128]{2,1,0:T(8,128)}) %reduce-scatter.2.cloned.1.call-update) | async-done | bytes 524304 | tf_op jit(solution)/shard_map/reduce_scatter | solution.py:43
  108.4 1.8 %convert_bitcast_fusion = (bf16[1,2,512,128]{3,2,1,0:T(8,128)(2,1)}, f32[2,512,128]{2,1,0:T(8,128)S(1)}) fusion(f32[2,512,128]{2,1,0:T(8,128)} %reduce-scatter.2.cloned.1.call-done, bf16[1,2,512,128]{3,2,1,0:T(8,128)(2,1)S(1)} %copy-done.2), kind=kLoop, calls=%fused_computation.28 | loop fusion | flops 393216 | bytes 1572864 | tf_op jit(solution)/shard_map/broadcast_in_dim | solution.py:48
  110.2 1.9 %fusion.25 = bf16[512,128]{1,0:T(8,128)(2,1)} fusion(f32[2,512,128]{2,1,0:T(8,128)S(1)} %get-tuple-element.4, f32[]{:T(128)} %bitcast.14, f32[]{:T(128)} %bitcast.13), kind=kLoop, calls=%fused_computation.32 | loop fusion | flops 262144 | bytes 655368 | tf_op jit(solution)/shard_map/convert_element_type | solution.py:47
  112.1 31.1 %all-reduce.2.cloned.1.call-done = bf16[512,128]{1,0:T(8,128)(2,1)} async-done(((bf16[512,128]{1,0:T(8,128)(2,1)}), bf16[512,128]{1,0:T(8,128)(2,1)}) %all-reduce.2.cloned.1.call-update) | async-done | bytes 131088 | tf_op jit(solution)/shard_map/psum | solution.py:47
  143.2 1.6 %convert_element_type.32 = f32[512,128]{1,0:T(8,128)} convert(bf16[512,128]{1,0:T(8,128)(2,1)} %all-reduce.2.cloned.1.call-done) | non-fusion elementwise | flops 65536 | bytes 393216 | tf_op jit(solution)/shard_map/convert_element_type | solution.py:47
  (15 shorter events, 0.1 us)
Async XLA Ops:
  7.2 53.8 %all-gather.2.cloned.1.call-start = ((), (), s32[]{:S(2)}) async-start(), calls=%async_computation.2 | async-start | bytes 1966080 | tf_op jit(solution)/shard_map/all_gather | solution.py:33
  9.6 13.9 %copy-start.1 = (bf16[1,2,4,96,192]{4,3,2,1,0:T(8,128)(2,1)S(1)}, bf16[1,2,4,96,192]{4,3,2,1,0:T(8,128)(2,1)}, u32[]{:S(2)}) copy-start(bf16[1,2,4,96,192]{4,3,2,1,0:T(8,128)(2,1)} %param.5) | copy-start | bytes 884740
  23.4 10.7 %copy-start = (bf16[1,2,2,96,512]{4,3,2,1,0:T(8,128)(2,1)S(1)}, bf16[1,2,2,96,512]{4,3,2,1,0:T(8,128)(2,1)}, u32[]{:S(2)}) copy-start(bf16[1,2,2,96,512]{4,3,2,1,0:T(8,128)(2,1)} %copy.14) | copy-start | bytes 1179652
  23.4 84.9 %reduce-scatter.2.cloned.1.call-start = ((), (), s32[]{:S(2)}) async-start(), calls=%async_computation.3 | async-start | bytes 2621440 | tf_op jit(solution)/shard_map/reduce_scatter | solution.py:43
  63.6 2.1 %copy-start.4 = (f32[384,512]{1,0:T(8,128)}, f32[384,512]{1,0:T(8,128)S(1)}, u32[]{:S(2)}) copy-start(f32[384,512]{1,0:T(8,128)S(1)} %fusion.4) | copy-start | bytes 2359300
  65.7 0.7 copy-start.3
  65.7 42.7 %copy-start.2 = (bf16[1,2,512,128]{3,2,1,0:T(8,128)(2,1)S(1)}, bf16[1,2,512,128]{3,2,1,0:T(8,128)(2,1)}, u32[]{:S(2)}) copy-start(bf16[1,2,512,128]{3,2,1,0:T(8,128)(2,1)} %param.8) | copy-start | bytes 786436
  65.7 77.5 %all-reduce.2.cloned.1.call-start = ((), (), s32[]{:S(2)}) async-start(), calls=%async_computation.4 | async-start | bytes 262144 | tf_op jit(solution)/shard_map/psum | solution.py:47
Sparse Core Ops, SparseCore 0:
  23.5 37.4 all-gather.1
  65.8 42.5 reduce-scatter.1
  112.2 30.9 all-reduce.1
where the time goes:
time: 152 us; the launch traced here: 151 us
  waiting for transfers between devices  99.4 us (65%)
  blocking collectives  22.7 us (15%)
  between operations  13.8 us (9%)
  other arithmetic  7.29 us (5%)
  local copies, waits for them, and re-layouts  4.86 us (3%)
  matrix products  3.19 us (2%)
    reduce_scatter x1, waiting for transfers between devices, body(): lax.psum_scatter(diag_terms, 'row', scatter_dimension=2, tiled=True)  41.4 us
    psum x1, waiting for transfers between devices, body(): lax.psum(density_term.astype(jnp.bfloat16), 'pole').astype(jnp.float32)  31.1 us
    all_gather x1, waiting for transfers between devices, body(): full_cols = lax.all_gather(local_rows, 'row', axis=2, tiled=True)  26.8 us
    all_to_all x1, blocking collectives, body(): lax.all_to_all(masked, 'col', split_axis=3, concat_axis=2, tiled=True)  12.2 us
    all_gather x1, blocking collectives, body(): segment = lax.all_gather(anc_inverse, 'col', axis=3, tiled=True)  10.5 us
    dot_general x2, matrix products, complex_left(): lax.dot_general(left_side, right_side, (((0,), (0,)), ((), ())), preferre...  3.19 us
  transfers between devices with their start and end apart: 3, of which 3 were waited for; matrix products, arithmetic and copies ran while one was open for 1% of the time, Pallas kernels for 0%

commit v1 on v0

v1 whole, which is shorter than its diff:
```python
import functools

import jax
import jax.numpy as jnp
from jax import lax
from jax.experimental import pallas as pl
from jax.experimental.pallas import tpu as pltpu
from jax.sharding import PartitionSpec as P

MESH = pl.DeviceIdType.MESH
F32 = jnp.float32
BF16 = jnp.bfloat16


def tdot(a, b):
    return lax.dot_general(a, b, (((0,), (0,)), ((), ())), preferred_element_type=F32)


def kernel(
    n_pole, n_row, n_col,
    anc, panel, pattern, diag_in, weight,
    inv_out, diag_out, dens,
    g, p, pm, acc, r_send, r_relay, r_full, s1_send, s1_recv, s2_send, s2_recv,
    loc_sem, ys, yr, gs, gr, zs, zr, fs, fr, rs, rr, ps, pr,
):
    me_p = lax.axis_index("pole")
    me_r = lax.axis_index("row")
    me_c = lax.axis_index("col")
    right = lax.rem(me_r + 1, n_row)
    left = lax.rem(me_r + n_row - 1, n_row)
    opp = lax.rem(me_r + 2, n_row)
    core = lax.rem(me_p, 2)
    partner = me_p + 1 - 2 * core
    n_x = n_pole // 2
    block = panel.shape[2]
    width = p.shape[2] // 2
    n_i = anc.shape[4]
    cols = r_send.shape[2] // 2

    def remote(src, dst, send, recv, **where):
        return pltpu.make_async_remote_copy(
            src_ref=src, dst_ref=dst, send_sem=send, recv_sem=recv, device_id=where, device_id_type=MESH)

    def hrows(h):
        return pl.ds(pl.multiple_of(h * block, 16), block)

    def pcols(o):
        return pl.ds(pl.multiple_of(o * width, 128), width)

    local = []
    for t in range(2):
        cp = pltpu.make_async_copy(
            panel.at[0, t, :, pcols(me_c)], p.at[me_r, hrows(me_c), pl.ds(t * width, width)], loc_sem.at[t])
        cp.start()
        local.append(cp)

    x_of = [lax.rem(me_p + 2 * j, n_pole) for j in range(1, n_x)]
    c_of = [lax.rem(me_c + j, n_col) for j in range(1, n_col)]
    barrier = pltpu.get_barrier_semaphore()
    peers = [{"row": right}, {"row": left}, {"pole": partner}]
    peers += [{"col": o} for o in c_of] + [{"pole": o} for o in x_of]
    for where in peers:
        pl.semaphore_signal(barrier, inc=1, device_id=where, device_id_type=MESH)

    for q in range(n_row):
        g[q, me_c] = jnp.concatenate([anc[0, 0, q], anc[0, 1, q]], axis=1)

    for cp in local:
        cp.wait()
    pl.semaphore_wait(barrier, len(peers))

    h_of = [lax.rem(me_c + n_col - k, n_col) for k in range(n_col)]
    y_copies, g_copies = {}, {}
    for j in range(1, n_col):
        for t in range(2):
            y_copies[j, t] = remote(
                panel.at[0, t, :, pcols(c_of[j - 1])], p.at[me_r, hrows(me_c), pl.ds(t * width, width)],
                ys.at[j - 1, t], yr.at[j - 1, t], col=c_of[j - 1])

    def z_pair(k):
        piece = p.at[me_r, hrows(h_of[k])]
        return (remote(piece, piece, zs.at[0, k], zr.at[0, k], row=right),
                remote(piece, piece, zs.at[1, k], zr.at[1, k], row=left))

    def f_pair(k):
        a = p.at[left, hrows(h_of[k]), pl.ds(0, width)]
        b = p.at[right, hrows(h_of[k]), pl.ds(width, width)]
        return (remote(a, a, fs.at[0, k], fr.at[0, k], row=right),
                remote(b, b, fs.at[1, k], fr.at[1, k], row=left))

    z_copies = [z_pair(k) for k in range(n_col)]
    f_copies = [f_pair(k) for k in range(n_col)]
    for k in range(n_col):
        for j in range(1, n_col):
            if k == 0:
                for t in range(2):
                    y_copies[j, t].start()
        if k > 0:
            y_copies[k, 0].wait_recv()
            y_copies[k, 1].wait_recv()
        for cp in z_copies[k]:
            cp.start()
    for j in range(1, n_col):
        g_copies[j] = remote(g.at[:, me_c], g.at[:, me_c], gs.at[j - 1], gr.at[j - 1], col=c_of[j - 1])
        g_copies[j].start()

    def mask_block(q):
        for h in range(n_col):
            keep = pattern[q * n_col + h, me_c].astype(F32)
            rows = pl.ds(h * block, block)
            pm[q, rows, :] = p[q, rows, :] * jnp.full((1, 2 * width), keep, F32).astype(BF16)

    m_all = 2 * n_i
    m_tile = m_all if m_all <= 512 else 384
    n_tile = 512

    def product(q, first):
        def tile(m0, n0):
            a = g[q, :, :, pl.ds(m0, m_tile)].reshape(n_col * block, m_tile)
            b = pm[q, :, pl.ds(n0, n_tile)]
            v = tdot(a, b)
            where = (pl.ds(m0, m_tile), pl.ds(n0, n_tile))
            acc[where] = v if first else acc[where] + v

        if m_all == m_tile:
            for n in range(2 * width // n_tile):
                tile(0, n * n_tile)
        else:
            @pl.loop(0, m_all // m_tile)
            def _(m):
                for n in range(2 * width // n_tile):
                    tile(pl.multiple_of(m * m_tile, 128), n * n_tile)

    mask_block(me_r)
    for k in range(n_col):
        z_copies[k][0].wait_recv()
        f_copies[k][0].start()
        z_copies[k][1].wait_recv()
        f_copies[k][1].start()
    mask_block(left)
    mask_block(right)
    for j in range(1, n_col):
        g_copies[j].wait_recv()
    product(me_r, True)
    product(left, False)
    product(right, False)
    for k in range(n_col):
        for cp in f_copies[k]:
            cp.wait_recv()
    mask_block(opp)
    product(opp, False)

    for s in range(n_row):
        re_cols = pl.ds(s * cols, cols)
        im_cols = pl.ds(width + s * cols, cols)
        re = acc[pl.ds(n_i, n_i), im_cols] - acc[pl.ds(0, n_i), re_cols]
        im = -(acc[pl.ds(n_i, n_i), re_cols] + acc[pl.ds(0, n_i), im_cols])
        inv_out[0, 0, :, re_cols] = re
        inv_out[0, 1, :, re_cols] = im
        r_send[s] = jnp.concatenate([re.astype(BF16), im.astype(BF16)], axis=1)
    r_full[me_r] = r_send[me_r]

    lo, hi = pl.ds(0, cols), pl.ds(cols, cols)
    first_leg = [
        remote(r_send.at[opp, :, lo], r_relay.at[0], rs.at[0], rr.at[0], row=right),
        remote(r_send.at[opp, :, hi], r_relay.at[1], rs.at[1], rr.at[1], row=left),
    ]
    direct = [
        remote(r_send.at[right], r_full.at[me_r], rs.at[2], rr.at[2], row=right),
        remote(r_send.at[left], r_full.at[me_r], rs.at[3], rr.at[3], row=left),
    ]
    second_leg = [
        remote(r_relay.at[0], r_full.at[left, :, lo], rs.at[4], rr.at[4], row=right),
        remote(r_relay.at[1], r_full.at[right, :, hi], rs.at[5], rr.at[5], row=left),
    ]
    for cp in first_leg + direct:
        cp.start()
    for a, b in zip(first_leg, second_leg):
        a.wait_recv()
        b.start()
    for cp in direct + second_leg:
        cp.wait_recv()

    half = width // 2
    w_re = weight[0, 0]
    w_im = weight[0, 1]

    def density_half(start):
        re = jnp.zeros((half, cols), F32)
        im = jnp.zeros((half, cols), F32)
        for q in range(n_row):
            r = r_full[q]
            a = tdot(pm[q, :, pl.ds(start, half)], r)
            b = tdot(pm[q, :, pl.ds(pl.multiple_of(width + start, 128), half)], r)
            re = re + a[:, :cols] - b[:, cols:]
            im = im + a[:, cols:] + b[:, :cols]
        rows = pl.ds(start, half)
        re = diag_in[0, 0, rows, :].astype(F32) - re
        im = diag_in[0, 1, rows, :].astype(F32) - im
        diag_out[0, 0, rows, :] = re.astype(BF16)
        diag_out[0, 1, rows, :] = im.astype(BF16)
        return w_re * im + w_im * re

    mine = pl.multiple_of(core * half, half)
    other = pl.multiple_of((1 - core) * half, half)
    s1_send[...] = density_half(other)
    swap = remote(s1_send, s1_recv, ps.at[0], pr.at[0], pole=partner)
    swap.start()
    own = density_half(mine)
    swap.wait_recv()
    s2_send[...] = (own + s1_recv[...]).astype(BF16)
    across = []
    for j in range(1, n_x):
        cp = remote(s2_send, s2_recv.at[j - 1], ps.at[1 + j], pr.at[1 + j], pole=x_of[j - 1])
        cp.start()
        across.append(cp)
    total = s2_send[...].astype(F32)
    for j in range(1, n_x):
        across[j - 1].wait_recv()
        total = total + s2_recv[j - 1].astype(F32)
    dens[pl.ds(mine, half), :] = total
    piece = dens.at[pl.ds(mine, half)]
    back = remote(piece, piece, ps.at[1], pr.at[1], pole=partner)
    back.start()
    back.wait_recv()

    sent = list(y_copies.values()) + list(g_copies.values())
    sent += [cp for pair in z_copies + f_copies for cp in pair]
    sent += first_leg + direct + second_leg + [swap, back] + across
    for cp in sent:
        cp.wait_send()


def body(n_pole, n_row, n_col, anc, panel, pattern, diag_in, weight):
    block = panel.shape[2]
    width = panel.shape[3] // n_col
    n_i = anc.shape[4]
    cols = diag_in.shape[3]
    n_x = n_pole // 2
    dma = pltpu.SemaphoreType.DMA
    vmem = pl.BlockSpec(memory_space=pltpu.VMEM)
    smem = pl.BlockSpec(memory_space=pltpu.SMEM)
    return pl.pallas_call(
        functools.partial(kernel, n_pole, n_row, n_col),
        out_shape=(
            jax.ShapeDtypeStruct((1, 2, n_i, width), F32),
            jax.ShapeDtypeStruct((1, 2, width, cols), BF16),
            jax.ShapeDtypeStruct((width, cols), F32),
        ),
        in_specs=[vmem, vmem, smem, vmem, smem],
        out_specs=(vmem, vmem, vmem),
        scratch_shapes=[
            pltpu.VMEM((n_row, n_col, block, 2 * n_i), BF16),
            pltpu.VMEM((n_row, n_col * block, 2 * width), BF16),
            pltpu.VMEM((n_row, n_col * block, 2 * width), BF16),
            pltpu.VMEM((2 * n_i, 2 * width), F32),
            pltpu.VMEM((n_row, n_i, 2 * cols), BF16),
            pltpu.VMEM((2, n_i, cols), BF16),
            pltpu.VMEM((n_row, n_i, 2 * cols), BF16),
            pltpu.VMEM((width // 2, cols), F32),
            pltpu.VMEM((width // 2, cols), F32),
            pltpu.VMEM((width // 2, cols), BF16),
            pltpu.VMEM((max(n_x - 1, 1), width // 2, cols), BF16),
            dma((2,)),
            dma((n_col - 1, 2)), dma((n_col - 1, 2)),
            dma((n_col - 1,)), dma((n_col - 1,)),
            dma((2, n_col)), dma((2, n_col)),
            dma((2, n_col)), dma((2, n_col)),
            dma((6,)), dma((6,)),
            dma((n_x + 1,)), dma((n_x + 1,)),
        ],
        compiler_params=pltpu.CompilerParams(
            collective_id=0, has_side_effects=True, vmem_limit_bytes=60 * 1024 * 1024),
        name="selinv",
    )(anc, panel, pattern, diag_in, weight)


def solution(mesh):
    shape = mesh.shape
    placed = (
        P("pole", None, None, "col", "row"),
        P("pole", None, ("row", "col"), None),
        P(),
        P("pole", None, "col", "row"),
        P("pole", None),
    )
    return jax.shard_map(
        functools.partial(body, shape["pole"], shape["row"], shape["col"]),
        mesh=mesh,
        in_specs=placed,
        out_specs=(P("pole", None, "row", "col"), P("pole", None, "col", "row"), P("col", "row")),
        check_vma=False,
    )
```

time: 152 us -> 57.6 us (0.38)
  waiting for transfers between devices: 99.4 us -> 0 us
  Pallas kernels: 0 us -> 51.6 us
  blocking collectives: 22.7 us -> 0 us
  between operations: 13.8 us -> 0.65 us
  other arithmetic: 7.29 us -> 0 us
  matrix products: 3.19 us -> 0 us
    pallas_call x0 -> x1, Pallas kernels: none -> 51.6 us  [body(): pl.pallas_call(functools.partial(kernel, n_pole, n_row, n_col), out_shape...]
    reduce_scatter x1 -> x0, waiting for transfers between devices: 41.4 us -> none  [body(): lax.psum_scatter(diag_terms, 'row', scatter_dimension=2, tiled=True)]
    psum x1 -> x0, waiting for transfers between devices: 31.1 us -> none  [body(): lax.psum(density_term.astype(jnp.bfloat16), 'pole').astype(jnp.float32)]
    all_gather x1 -> x0, waiting for transfers between devices: 26.8 us -> none  [body(): full_cols = lax.all_gather(local_rows, 'row', axis=2, tiled=True)]
    all_to_all x1 -> x0, blocking collectives: 12.2 us -> none  [body(): lax.all_to_all(masked, 'col', split_axis=3, concat_axis=2, tiled=True)]
    all_gather x1 -> x0, blocking collectives: 10.5 us -> none  [body(): segment = lax.all_gather(anc_inverse, 'col', axis=3, tiled=True)]
    unnamed x12 -> x8, local copies, waits for them, and re-layouts: 0.68 us -> 5.2 us
    convert_element_type x3 -> x0, other arithmetic: 4.38 us -> none  [the longest x1 1.89 us: body(): density_term.astype(jnp.bfloat16)]
  transfers between devices with their start and end apart: 3 -> 0, of which waited for: 3 -> 0; matrix products, arithmetic and copies ran while one was open for 1% -> 0% of each run, Pallas kernels for 0% -> 0%
where the time goes in v1:
time: 57.6 us; the launch traced here: 57.4 us
  Pallas kernels  51.6 us (90%)
  local copies, waits for them, and re-layouts  5.2 us (9%)
  between operations  0.65 us (1%)
    pallas_call x1, Pallas kernels, body(): pl.pallas_call(functools.partial(kernel, n_pole, n_row, n_col), out_shape...  51.6 us
    unnamed x8, local copies, waits for them, and re-layouts  5.2 us

profile of v1, /device:TPU:0, one launch (start us, length us, event | category | flops | bytes accessed | tf_op | source)
XLA Modules:
  0.0 57.4 jit_solution(6202161499425890221)
XLA Ops:
  0.6 1.3 %copy.8.pattern = s32[8,2]{1,0:T(8,128)} copy(s32[8,2]{0,1:T(2,128)} %param.7) | data formatting | bytes 128 | tf_op args[2]
  2.0 51.6 %selinv.1 = (f32[1,2,192,512]{3,2,1,0:T(8,128)}, bf16[1,2,512,128]{3,2,1,0:T(8,128)(2,1)}, f32[512,128]{1,0:T(8,128)}) custom-call(bf16[1,2,4,96,192]{4,3,2,1,0:T(8,128)(2,1)} %anc.1, bf16[1,2,96,1024]{3,2,1,0:T(8,128)(2,1)} %panel.1, s32[8,2]{1,0:T(8,128)} %copy.8.pattern, bf16[1,2,512,128]{3,2,1,0:T(8,128)(2,1)} %diag_in.1, f32[1,2]{1,0:T(1,128)} %weight.1), custom_call_target="tpu_custom_call" | custom-call | tf_op jit(solution)/shard_map/selinv/pallas_call | solution.py:243
  53.6 0.0 copy-start.1
  53.6 2.1 %copy.12 = f32[1,2,192,512]{3,2,1,0:T(8,128)} copy(f32[1,2,192,512]{3,2,1,0:T(8,128)} %get-tuple-element.6) | data formatting | bytes 1572864
  55.7 0.0 copy-done.1
  55.7 0.0 copy-start
  55.7 0.7 %copy.13 = bf16[1,2,512,128]{3,2,1,0:T(8,128)(2,1)} copy(bf16[1,2,512,128]{3,2,1,0:T(8,128)(2,1)S(1)} %copy-done.1) | data formatting | bytes 524288
  56.4 0.3 copy-done
  56.7 0.7 %copy.14 = f32[512,128]{1,0:T(8,128)} copy(f32[512,128]{1,0:T(8,128)S(1)} %copy-done) | data formatting | bytes 524288
Async XLA Ops:
  53.6 2.1 %copy-start.1 = (bf16[1,2,512,128]{3,2,1,0:T(8,128)(2,1)S(1)}, bf16[1,2,512,128]{3,2,1,0:T(8,128)(2,1)}, u32[]{:S(2)}) copy-start(bf16[1,2,512,128]{3,2,1,0:T(8,128)(2,1)} %get-tuple-element.7) | copy-start | bytes 786436
  55.7 1.0 %copy-start = (f32[512,128]{1,0:T(8,128)S(1)}, f32[512,128]{1,0:T(8,128)}, u32[]{:S(2)}) copy-start(f32[512,128]{1,0:T(8,128)} %get-tuple-element.8) | copy-start | bytes 786436

commit v2 on v1

--- a/solution.py
+++ b/solution.py
@@ -20,15 +20,14 @@
     n_pole, n_row, n_col,
     anc, panel, pattern, diag_in, weight,
     inv_out, diag_out, dens,
-    g, p, pm, acc, r_send, r_relay, r_full, s1_send, s1_recv, s2_send, s2_recv,
-    loc_sem, ys, yr, gs, gr, zs, zr, fs, fr, rs, rr, ps, pr,
+    g, p, pm, acc, r_send, r_full, s1_send, s1_recv, s2_send, s2_recv,
+    loc_sem, ys, yr, gs, gr, zs, zr, rs, rr, ps, pr,
 ):
     me_p = lax.axis_index("pole")
     me_r = lax.axis_index("row")
     me_c = lax.axis_index("col")
     right = lax.rem(me_r + 1, n_row)
     left = lax.rem(me_r + n_row - 1, n_row)
-    opp = lax.rem(me_r + 2, n_row)
     core = lax.rem(me_p, 2)
     partner = me_p + 1 - 2 * core
     n_x = n_pole // 2
@@ -57,7 +56,8 @@
     x_of = [lax.rem(me_p + 2 * j, n_pole) for j in range(1, n_x)]
     c_of = [lax.rem(me_c + j, n_col) for j in range(1, n_col)]
     barrier = pltpu.get_barrier_semaphore()
-    peers = [{"row": right}, {"row": left}, {"pole": partner}]
+    r_of = [lax.rem(me_r + j, n_row) for j in range(1, n_row)]
+    peers = [{"pole": partner}] + [{"row": o} for o in r_of]
     peers += [{"col": o} for o in c_of] + [{"pole": o} for o in x_of]
     for where in peers:
         pl.semaphore_signal(barrier, inc=1, device_id=where, device_id_type=MESH)
@@ -77,38 +77,51 @@
                 panel.at[0, t, :, pcols(c_of[j - 1])], p.at[me_r, hrows(me_c), pl.ds(t * width, width)],
                 ys.at[j - 1, t], yr.at[j - 1, t], col=c_of[j - 1])
 
-    def z_pair(k):
-        piece = p.at[me_r, hrows(h_of[k])]
-        return (remote(piece, piece, zs.at[0, k], zr.at[0, k], row=right),
-                remote(piece, piece, zs.at[1, k], zr.at[1, k], row=left))
-
-    def f_pair(k):
-        a = p.at[left, hrows(h_of[k]), pl.ds(0, width)]
-        b = p.at[right, hrows(h_of[k]), pl.ds(width, width)]
-        return (remote(a, a, fs.at[0, k], fr.at[0, k], row=right),
-                remote(b, b, fs.at[1, k], fr.at[1, k], row=left))
-
-    z_copies = [z_pair(k) for k in range(n_col)]
-    f_copies = [f_pair(k) for k in range(n_col)]
+    last = n_row - 1
+
+    def moving_right(d, k):
+        piece = p.at[lax.rem(me_r + n_row - (d - 1), n_row), hrows(h_of[k])]
+        return remote(piece, piece, zs.at[0, d - 1, k], zr.at[0, d - 1, k], row=right)
+
+    def moving_left(d, k):
+        piece = p.at[lax.rem(me_r + d - 1, n_row), hrows(h_of[k])]
+        return remote(piece, piece, zs.at[1, d - 1, k], zr.at[1, d - 1, k], row=left)
+
+    def from_left(d, k):
+        piece = p.at[lax.rem(me_r + n_row - d, n_row), hrows(h_of[k])]
+        return remote(piece, piece, zs.at[0, d - 1, k], zr.at[0, d - 1, k], row=right)
+
+    def from_right(d, k):
+        piece = p.at[lax.rem(me_r + d, n_row), hrows(h_of[k])]
+        return remote(piece, piece, zs.at[1, d - 1, k], zr.at[1, d - 1, k], row=left)
+
     for k in range(n_col):
-        for j in range(1, n_col):
-            if k == 0:
-                for t in range(2):
-                    y_copies[j, t].start()
-        if k > 0:
+        if k == 0:
+            for cp in y_copies.values():
+                cp.start()
+        else:
             y_copies[k, 0].wait_recv()
             y_copies[k, 1].wait_recv()
-        for cp in z_copies[k]:
-            cp.start()
+
+        @pl.when(me_r < last)
+        def _():
+            moving_right(1, k).start()
+
+        @pl.when(me_r > 0)
+        def _():
+            moving_left(1, k).start()
+
     for j in range(1, n_col):
         g_copies[j] = remote(g.at[:, me_c], g.at[:, me_c], gs.at[j - 1], gr.at[j - 1], col=c_of[j - 1])
         g_copies[j].start()
 
     def mask_block(q):
         for h in range(n_col):
-            keep = pattern[q * n_col + h, me_c].astype(F32)
+            row = pattern[pl.ds(q * n_col + h, 1), :].astype(F32)
+            lane = lax.broadcasted_iota(jnp.int32, row.shape, 1)
+            keep = jnp.sum(jnp.where(lane == me_c, row, 0.0), axis=1, keepdims=True)
             rows = pl.ds(h * block, block)
-            pm[q, rows, :] = p[q, rows, :] * jnp.full((1, 2 * width), keep, F32).astype(BF16)
+            pm[q, rows, :] = p[q, rows, :] * jnp.broadcast_to(keep, (1, 2 * width)).astype(BF16)
 
     m_all = 2 * n_i
     m_tile = m_all if m_all <= 512 else 384
@@ -132,53 +145,59 @@
                     tile(pl.multiple_of(m * m_tile, 128), n * n_tile)
 
     mask_block(me_r)
-    for k in range(n_col):
-        z_copies[k][0].wait_recv()
-        f_copies[k][0].start()
-        z_copies[k][1].wait_recv()
-        f_copies[k][1].start()
-    mask_block(left)
-    mask_block(right)
-    for j in range(1, n_col):
-        g_copies[j].wait_recv()
-    product(me_r, True)
-    product(left, False)
-    product(right, False)
-    for k in range(n_col):
-        for cp in f_copies[k]:
-            cp.wait_recv()
-    mask_block(opp)
-    product(opp, False)
+    for d in range(1, n_row):
+        for k in range(n_col):
+            @pl.when(me_r >= d)
+            def _():
+                from_left(d, k).wait_recv()
+
+                @pl.when(me_r < last)
+                def _():
+                    moving_right(d + 1, k).start()
+
+            @pl.when(me_r <= last - d)
+            def _():
+                from_right(d, k).wait_recv()
+
+                @pl.when(me_r > 0)
+                def _():
+                    moving_left(d + 1, k).start()
+
+        if d == 1:
+            for cp in g_copies.values():
+                cp.wait_recv()
+            product(me_r, True)
+
+        @pl.when(me_r >= d)
+        def _():
+            q = lax.rem(me_r + n_row - d, n_row)
+            mask_block(q)
+            product(q, False)
+
+        @pl.when(me_r <= last - d)
+        def _():
+            q = lax.rem(me_r + d, n_row)
+            mask_block(q)
+            product(q, False)
 
     for s in range(n_row):
         re_cols = pl.ds(s * cols, cols)
         im_cols = pl.ds(width + s * cols, cols)
         re = acc[pl.ds(n_i, n_i), im_cols] - acc[pl.ds(0, n_i), re_cols]
         im = -(acc[pl.ds(n_i, n_i), re_cols] + acc[pl.ds(0, n_i), im_cols])
-        inv_out[0, 0, :, re_cols] = re
-        inv_out[0, 1, :, re_cols] = im
+        inv_out[0, 0, :, re_cols] = re.astype(BF16)
+        inv_out[0, 1, :, re_cols] = im.astype(BF16)
         r_send[s] = jnp.concatenate([re.astype(BF16), im.astype(BF16)], axis=1)
     r_full[me_r] = r_send[me_r]
 
-    lo, hi = pl.ds(0, cols), pl.ds(cols, cols)
-    first_leg = [
-        remote(r_send.at[opp, :, lo], r_relay.at[0], rs.at[0], rr.at[0], row=right),
-        remote(r_send.at[opp, :, hi], r_relay.at[1], rs.at[1], rr.at[1], row=left),
+    order = [2, 3, 1] if n_row == 4 else list(range(1, n_row))
+    direct = [
+        remote(r_send.at[r_of[j - 1]], r_full.at[me_r], rs.at[j - 1], rr.at[j - 1], row=r_of[j - 1])
+        for j in order
     ]
-    direct = [
-        remote(r_send.at[right], r_full.at[me_r], rs.at[2], rr.at[2], row=right),
-        remote(r_send.at[left], r_full.at[me_r], rs.at[3], rr.at[3], row=left),
-    ]
-    second_leg = [
-        remote(r_relay.at[0], r_full.at[left, :, lo], rs.at[4], rr.at[4], row=right),
-        remote(r_relay.at[1], r_full.at[right, :, hi], rs.at[5], rr.at[5], row=left),
-    ]
-    for cp in first_leg + direct:
+    for cp in direct:
         cp.start()
-    for a, b in zip(first_leg, second_leg):
-        a.wait_recv()
-        b.start()
-    for cp in direct + second_leg:
+    for cp in direct:
         cp.wait_recv()
 
     half = width // 2
@@ -225,10 +244,18 @@
     back.wait_recv()
 
     sent = list(y_copies.values()) + list(g_copies.values())
-    sent += [cp for pair in z_copies + f_copies for cp in pair]
-    sent += first_leg + direct + second_leg + [swap, back] + across
+    sent += direct + [swap, back] + across
     for cp in sent:
         cp.wait_send()
+    for d in range(1, n_row):
+        for k in range(n_col):
+            @pl.when((me_r < last) & (me_r >= d - 1))
+            def _():
+                moving_right(d, k).wait_send()
+
+            @pl.when((me_r > 0) & (me_r <= last - (d - 1)))
+            def _():
+                moving_left(d, k).wait_send()
 
 
 def body(n_pole, n_row, n_col, anc, panel, pattern, diag_in, weight):
@@ -240,14 +267,14 @@
     dma = pltpu.SemaphoreType.DMA
     vmem = pl.BlockSpec(memory_space=pltpu.VMEM)
     smem = pl.BlockSpec(memory_space=pltpu.SMEM)
-    return pl.pallas_call(
+    inv, diag, dens = pl.pallas_call(
         functools.partial(kernel, n_pole, n_row, n_col),
         out_shape=(
-            jax.ShapeDtypeStruct((1, 2, n_i, width), F32),
+            jax.ShapeDtypeStruct((1, 2, n_i, width), BF16),
             jax.ShapeDtypeStruct((1, 2, width, cols), BF16),
             jax.ShapeDtypeStruct((width, cols), F32),
         ),
-        in_specs=[vmem, vmem, smem, vmem, smem],
+        in_specs=[vmem, vmem, vmem, vmem, smem],
         out_specs=(vmem, vmem, vmem),
         scratch_shapes=[
             pltpu.VMEM((n_row, n_col, block, 2 * n_i), BF16),
@@ -255,7 +282,6 @@
             pltpu.VMEM((n_row, n_col * block, 2 * width), BF16),
             pltpu.VMEM((2 * n_i, 2 * width), F32),
             pltpu.VMEM((n_row, n_i, 2 * cols), BF16),
-            pltpu.VMEM((2, n_i, cols), BF16),
             pltpu.VMEM((n_row, n_i, 2 * cols), BF16),
             pltpu.VMEM((width // 2, cols), F32),
             pltpu.VMEM((width // 2, cols), F32),
@@ -264,15 +290,15 @@
             dma((2,)),
             dma((n_col - 1, 2)), dma((n_col - 1, 2)),
             dma((n_col - 1,)), dma((n_col - 1,)),
-            dma((2, n_col)), dma((2, n_col)),
-            dma((2, n_col)), dma((2, n_col)),
-            dma((6,)), dma((6,)),
+            dma((2, n_row - 1, n_col)), dma((2, n_row - 1, n_col)),
+            dma((n_row - 1,)), dma((n_row - 1,)),
             dma((n_x + 1,)), dma((n_x + 1,)),
         ],
         compiler_params=pltpu.CompilerParams(
             collective_id=0, has_side_effects=True, vmem_limit_bytes=60 * 1024 * 1024),
         name="selinv",
     )(anc, panel, pattern, diag_in, weight)
+    return inv.astype(F32), diag, dens
 
 
 def solution(mesh):

time: 57.6 us -> 57.5 us (level)
  local copies, waits for them, and re-layouts: 5.2 us -> 3.1 us
  other arithmetic: 0 us -> 2.01 us
    unnamed x8 -> x7, local copies, waits for them, and re-layouts: 5.2 us -> 3.1 us
    convert_element_type x0 -> x1, other arithmetic: none -> 2.01 us  [body(): return (inv.astype(F32), diag, dens)]
where the time goes in v2:
time: 57.5 us; the launch traced here: 57.3 us
  Pallas kernels  51.6 us (90%)
  local copies, waits for them, and re-layouts  3.1 us (5%)
  other arithmetic  2.01 us (3%)
  between operations  0.65 us (1%)
    pallas_call x1, Pallas kernels, body(): pl.pallas_call(functools.partial(kernel, n_pole, n_row, n_col), out_shape...  51.6 us
    unnamed x7, local copies, waits for them, and re-layouts  3.1 us
    convert_element_type x1, other arithmetic, body(): return (inv.astype(F32), diag, dens)  2.01 us

profile of v2, /device:TPU:0, one launch (start us, length us, event | category | flops | bytes accessed | tf_op | source)
XLA Modules:
  0.0 57.3 jit_solution(16334520240918342708)
XLA Ops:
  0.6 1.3 %copy.8.pattern = s32[8,2]{1,0:T(8,128)} copy(s32[8,2]{0,1:T(2,128)} %param.7) | data formatting | bytes 128 | tf_op args[2]
  2.0 51.6 %selinv.1 = (bf16[1,2,192,512]{3,2,1,0:T(8,128)(2,1)}, bf16[1,2,512,128]{3,2,1,0:T(8,128)(2,1)}, f32[512,128]{1,0:T(8,128)}) custom-call(bf16[1,2,4,96,192]{4,3,2,1,0:T(8,128)(2,1)} %anc.1, bf16[1,2,96,1024]{3,2,1,0:T(8,128)(2,1)} %panel.1, s32[8,2]{1,0:T(8,128)} %copy.8.pattern, bf16[1,2,512,128]{3,2,1,0:T(8,128)(2,1)} %diag_in.1, f32[1,2]{1,0:T(1,128)} %weight.1), custom_call_target="tpu_custom_call" | custom-call | tf_op jit(solution)/shard_map/selinv/pallas_call | solution.py:270
  53.5 0.0 copy-start.1
  53.6 2.0 %convert_element_type.3 = f32[1,2,192,512]{3,2,1,0:T(8,128)} convert(bf16[1,2,192,512]{3,2,1,0:T(8,128)(2,1)} %get-tuple-element.6) | non-fusion elementwise | flops 196608 | bytes 1179648 | tf_op jit(solution)/shard_map/convert_element_type | solution.py:301
  55.6 0.0 copy-done.1
  55.6 0.0 copy-start
  55.6 0.7 %copy.11 = bf16[1,2,512,128]{3,2,1,0:T(8,128)(2,1)} copy(bf16[1,2,512,128]{3,2,1,0:T(8,128)(2,1)S(1)} %copy-done.1) | data formatting | bytes 524288
  56.3 0.3 copy-done
  56.6 0.7 %copy.12 = f32[512,128]{1,0:T(8,128)} copy(f32[512,128]{1,0:T(8,128)S(1)} %copy-done) | data formatting | bytes 524288
Async XLA Ops:
  53.5 2.0 %copy-start.1 = (bf16[1,2,512,128]{3,2,1,0:T(8,128)(2,1)S(1)}, bf16[1,2,512,128]{3,2,1,0:T(8,128)(2,1)}, u32[]{:S(2)}) copy-start(bf16[1,2,512,128]{3,2,1,0:T(8,128)(2,1)} %get-tuple-element.13) | copy-start | bytes 786436
  55.6 1.0 %copy-start = (f32[512,128]{1,0:T(8,128)S(1)}, f32[512,128]{1,0:T(8,128)}, u32[]{:S(2)}) copy-start(f32[512,128]{1,0:T(8,128)} %get-tuple-element.14) | copy-start | bytes 786436

commit v3 on v2

--- a/solution.py
+++ b/solution.py
@@ -80,28 +80,27 @@
     last = n_row - 1
 
     def moving_right(d, k):
-        piece = p.at[lax.rem(me_r + n_row - (d - 1), n_row), hrows(h_of[k])]
+        piece = p.at[lax.rem(me_r + n_row - (d - 1), n_row), hrows(h_of[k // 2]), pl.ds(k % 2 * width, width)]
         return remote(piece, piece, zs.at[0, d - 1, k], zr.at[0, d - 1, k], row=right)
 
     def moving_left(d, k):
-        piece = p.at[lax.rem(me_r + d - 1, n_row), hrows(h_of[k])]
+        piece = p.at[lax.rem(me_r + d - 1, n_row), hrows(h_of[k // 2]), pl.ds(k % 2 * width, width)]
         return remote(piece, piece, zs.at[1, d - 1, k], zr.at[1, d - 1, k], row=left)
 
     def from_left(d, k):
-        piece = p.at[lax.rem(me_r + n_row - d, n_row), hrows(h_of[k])]
+        piece = p.at[lax.rem(me_r + n_row - d, n_row), hrows(h_of[k // 2]), pl.ds(k % 2 * width, width)]
         return remote(piece, piece, zs.at[0, d - 1, k], zr.at[0, d - 1, k], row=right)
 
     def from_right(d, k):
-        piece = p.at[lax.rem(me_r + d, n_row), hrows(h_of[k])]
+        piece = p.at[lax.rem(me_r + d, n_row), hrows(h_of[k // 2]), pl.ds(k % 2 * width, width)]
         return remote(piece, piece, zs.at[1, d - 1, k], zr.at[1, d - 1, k], row=left)
 
-    for k in range(n_col):
+    for k in range(2 * n_col):
         if k == 0:
             for cp in y_copies.values():
                 cp.start()
-        else:
-            y_copies[k, 0].wait_recv()
-            y_copies[k, 1].wait_recv()
+        if k >= 2:
+            y_copies[k // 2, k % 2].wait_recv()
 
         @pl.when(me_r < last)
         def _():
@@ -146,7 +145,7 @@
 
     mask_block(me_r)
     for d in range(1, n_row):
-        for k in range(n_col):
+        for k in range(2 * n_col):
             @pl.when(me_r >= d)
             def _():
                 from_left(d, k).wait_recv()
@@ -248,7 +247,7 @@
     for cp in sent:
         cp.wait_send()
     for d in range(1, n_row):
-        for k in range(n_col):
+        for k in range(2 * n_col):
             @pl.when((me_r < last) & (me_r >= d - 1))
             def _():
                 moving_right(d, k).wait_send()
@@ -290,7 +289,7 @@
             dma((2,)),
             dma((n_col - 1, 2)), dma((n_col - 1, 2)),
             dma((n_col - 1,)), dma((n_col - 1,)),
-            dma((2, n_row - 1, n_col)), dma((2, n_row - 1, n_col)),
+            dma((2, n_row - 1, 2 * n_col)), dma((2, n_row - 1, 2 * n_col)),
             dma((n_row - 1,)), dma((n_row - 1,)),
             dma((n_x + 1,)), dma((n_x + 1,)),
         ],

time: 57.5 us -> 56.7 us (0.986)
  Pallas kernels: 51.6 us -> 50.7 us
    pallas_call x1, Pallas kernels: 51.6 us -> 50.7 us  [body(): pl.pallas_call(functools.partial(kernel, n_pole, n_row, n_col), out_shape...]
where the time goes in v3:
time: 56.7 us; the launch traced here: 56.5 us
  Pallas kernels  50.7 us (89%)
  local copies, waits for them, and re-layouts  3.1 us (5%)
  other arithmetic  2.01 us (4%)
  between operations  0.65 us (1%)
    pallas_call x1, Pallas kernels, body(): pl.pallas_call(functools.partial(kernel, n_pole, n_row, n_col), out_shape...  50.7 us
    unnamed x7, local copies, waits for them, and re-layouts  3.1 us
    convert_element_type x1, other arithmetic, body(): return (inv.astype(F32), diag, dens)  2.01 us

profile of v3, /device:TPU:0, one launch (start us, length us, event | category | flops | bytes accessed | tf_op | source)
XLA Modules:
  0.0 56.5 jit_solution(13619413840584257986)
XLA Ops:
  0.6 1.3 %copy.8.pattern = s32[8,2]{1,0:T(8,128)} copy(s32[8,2]{0,1:T(2,128)} %param.7) | data formatting | bytes 128 | tf_op args[2]
  2.0 50.7 %selinv.1 = (bf16[1,2,192,512]{3,2,1,0:T(8,128)(2,1)}, bf16[1,2,512,128]{3,2,1,0:T(8,128)(2,1)}, f32[512,128]{1,0:T(8,128)}) custom-call(bf16[1,2,4,96,192]{4,3,2,1,0:T(8,128)(2,1)} %anc.1, bf16[1,2,96,1024]{3,2,1,0:T(8,128)(2,1)} %panel.1, s32[8,2]{1,0:T(8,128)} %copy.8.pattern, bf16[1,2,512,128]{3,2,1,0:T(8,128)(2,1)} %diag_in.1, f32[1,2]{1,0:T(1,128)} %weight.1), custom_call_target="tpu_custom_call" | custom-call | tf_op jit(solution)/shard_map/selinv/pallas_call | solution.py:269
  52.7 0.0 copy-start.1
  52.7 2.0 %convert_element_type.3 = f32[1,2,192,512]{3,2,1,0:T(8,128)} convert(bf16[1,2,192,512]{3,2,1,0:T(8,128)(2,1)} %get-tuple-element.6) | non-fusion elementwise | flops 196608 | bytes 1179648 | tf_op jit(solution)/shard_map/convert_element_type | solution.py:300
  54.7 0.0 copy-done.1
  54.7 0.0 copy-start
  54.7 0.7 %copy.11 = bf16[1,2,512,128]{3,2,1,0:T(8,128)(2,1)} copy(bf16[1,2,512,128]{3,2,1,0:T(8,128)(2,1)S(1)} %copy-done.1) | data formatting | bytes 524288
  55.4 0.3 copy-done
  55.8 0.7 %copy.12 = f32[512,128]{1,0:T(8,128)} copy(f32[512,128]{1,0:T(8,128)S(1)} %copy-done) | data formatting | bytes 524288
Async XLA Ops:
  52.7 2.0 %copy-start.1 = (bf16[1,2,512,128]{3,2,1,0:T(8,128)(2,1)S(1)}, bf16[1,2,512,128]{3,2,1,0:T(8,128)(2,1)}, u32[]{:S(2)}) copy-start(bf16[1,2,512,128]{3,2,1,0:T(8,128)(2,1)} %get-tuple-element.13) | copy-start | bytes 786436
  54.7 1.0 %copy-start = (f32[512,128]{1,0:T(8,128)S(1)}, f32[512,128]{1,0:T(8,128)}, u32[]{:S(2)}) copy-start(f32[512,128]{1,0:T(8,128)} %get-tuple-element.14) | copy-start | bytes 786436
